TPU v7x, 32 devices: a whole 2x2x4 slice. The times are simulated.
32 devices in a mesh: section: 4 (over y, x), dp: 8 (over z, core).
Axes of the slice: x: 2, y: 2, z: 4, core: 2. Of those that a mesh axis runs over, the one named last changes fastest.
Arguments:
- inputs: bfloat16 [8, 128, 16384], P(None, None, 'dp'), may hold values from -6 to 6
- cotangent: bfloat16 [4, 8, 128, 1024], P('section'), may hold values from -0.5 to 0.5
- norm_gain: bfloat16 [4, 16384], P('section', 'dp'), may hold values from 0.099609375 to 1.8984375
- value_weight: bfloat16 [4, 16384, 1024], P('section', 'dp'), may hold values from -0.046875 to 0.046875
- output_weight: bfloat16 [4, 1024, 16384], P('section', None, 'dp'), may hold values from -0.1875 to 0.1875
- left_old: float32 [4, 16, 1024, 1024], P('section', 'dp'), may hold values from -0.4 to 2.4, as said below
- right_old: float32 [4, 1024, 1024], P('section', 'dp'), may hold values from -0.4 to 2.4, as said below
Outputs:
- section_outputs: bfloat16 [4, 8, 128, 16384], P('section', None, None, 'dp')
- left_stats: float32 [4, 16, 1024, 1024], P('section', 'dp')
- right_stats: float32 [4, 1024, 1024], P('section', 'dp')
Inputs may be any that keep to these rules, and one draw needn't show every extreme that they name: `left_old`: symmetric in its last two dimensions. `right_old`: symmetric in its last two dimensions.
All inputs are finite; a program needn't handle non-finite values.
Results may differ from a plain program's by a relative error of at most 0.015.
Values may be sent and summed in bfloat16 or wider, within the bound.
A program may use at most 128 MiB of HBM per device.

v0:
```python
import functools

import jax
import jax.numpy as jnp
from jax import lax
from jax.experimental import pallas as pl
from jax.experimental.pallas import tpu as pltpu
from jax.sharding import PartitionSpec as P

BLOCK = 1024
MESH = pl.DeviceIdType.MESH
F32 = jnp.float32
BF16 = jnp.bfloat16


def relay_kernel(
    sections, dp, model_width,
    x_in, cot_in, gain, wv_in, wo_in,
    *refs,
):
    chips = dp // 2
    out_hbm, grad = refs[:2]
    parts = refs[2:2 + chips]
    (
        out, scaled, weighted, cot, wv, wo, acc, right_own, right_send, right_recv,
        xbuf, prod, csum, invs, sq, pair_send, pair_recv, rs_send, rs_recv, vals,
        send_sem, recv_sem, load_sem, store_sem, right_sem,
    ) = refs[2 + chips:]
    micro, rows_all, cols = x_in.shape
    width = wv.shape[1]
    half = rows_all // 2
    rows = half // chips
    share = width // dp
    s = lax.axis_index("section")
    d = lax.axis_index("dp")
    z = d // 2
    c = lax.rem(d, 2)
    partner = z * 2 + (1 - c)

    def device(section, index):
        return (section, index)

    loads = [
        pltpu.make_async_copy(src, dst, load_sem.at[i])
        for i, (src, dst) in enumerate(((wv_in, wv), (cot_in, cot), (wo_in, wo)))
    ]

    @pl.when(s == 0)
    def _():
        pltpu.make_async_copy(x_in.at[0], xbuf.at[0], recv_sem.at[0, 0]).start()

    for load in loads:
        load.start()

    @pl.when(s == 0)
    def _():
        @pl.loop(1, micro)
        def _(m):
            pltpu.make_async_copy(x_in.at[m], xbuf.at[m], recv_sem.at[0, m]).start()

    barrier = pltpu.get_barrier_semaphore()
    for j in range(1, dp):
        pl.semaphore_signal(barrier, inc=1, device_id=device(s, lax.rem(d + j, dp)), device_id_type=MESH)

    @pl.when(s > 0)
    def _():
        pl.semaphore_signal(barrier, inc=1, device_id=device(s - 1, d), device_id_type=MESH)

    @pl.when(s < sections - 1)
    def _():
        pl.semaphore_signal(barrier, inc=1, device_id=device(s + 1, d), device_id_type=MESH)

    pl.semaphore_wait(
        barrier, dp - 1 + jnp.minimum(s, 1) + jnp.minimum(sections - 1 - s, 1)
    )

    def send(src, dst, phase, m, section, index):
        pltpu.make_async_remote_copy(
            src_ref=src, dst_ref=dst,
            send_sem=send_sem.at[phase, m], recv_sem=recv_sem.at[phase, m],
            device_id=device(section, index), device_id_type=MESH,
        ).start()

    def wait_in(ref, phase, m):
        pltpu.make_async_copy(ref, ref, recv_sem.at[phase, m]).wait()

    def wait_out(ref, phase, m):
        pltpu.make_async_copy(ref, ref, send_sem.at[phase, m]).wait()

    def step_project(m):
        wait_in(xbuf.at[m], 0, m)
        total = jnp.zeros((rows_all, 128), F32)
        for k in range(cols // 128):
            piece = xbuf[m, :, k * 128:(k + 1) * 128].astype(F32)
            total = total + piece * piece
            scaled[m, :, k * 128:(k + 1) * 128] = (
                piece * gain[:, k * 128:(k + 1) * 128].astype(F32)
            ).astype(BF16)
        row = jnp.sum(total.T, axis=0, keepdims=True)
        sq[m, d] = jnp.broadcast_to(row, (8, rows_all))
        for j in range(1, dp):
            send(sq.at[m, d], sq.at[m, d], 1, m, s, lax.rem(d + j, dp))

        @pl.when(m == 0)
        def _():
            loads[0].wait()

        @pl.loop(0, width // 256)
        def _(n):
            at = pl.ds(pl.multiple_of(n * 256, 256), 256)
            prod[:, at] = jnp.dot(scaled[m], wv[:, at], preferred_element_type=F32)

        pair_send[m] = prod[pl.ds(pl.multiple_of((1 - c) * half, half), half), :].astype(BF16)
        send(pair_send.at[m], pair_recv.at[m], 2, m, s, partner)

    def step_forward(m):
        wait_in(vals.at[m, c, pl.ds(0, chips - 1)], 4, m)
        send(vals.at[m, c], vals.at[m, c], 5, m, s, partner)

    def step_scatter(m):
        wait_in(pair_recv.at[m], 2, m)
        csum[...] = prod[pl.ds(pl.multiple_of(c * half, half), half), :] + pair_recv[m].astype(F32)
        for j in range(1, chips):
            target = lax.rem(z + j, chips)
            rs_send[m, j - 1] = csum[pl.ds(pl.multiple_of(target * rows, rows), rows), :].astype(BF16)
            send(rs_send.at[m, j - 1], rs_recv.at[m, chips - 1 - j], 3, m, s, target * 2 + c)

    def step_output(m):
        wait_in(vals.at[m, 1 - c], 5, m)

        @pl.when(m == 0)
        def _():
            loads[2].wait()

        values = vals[m].reshape(rows_all, width)

        for side in range(2):
            @pl.loop(0, cols // 1024)
            def _(n):
                at = pl.ds(pl.multiple_of(side * (cols // 2) + n * 512, 512), 512)
                out[m, :, at] = (
                    xbuf[m, :, at].astype(F32)
                    + jnp.dot(values, wo[:, at], preferred_element_type=F32)
                ).astype(BF16)

            cut = pl.ds(side * (cols // 2), cols // 2)

            @pl.when(s < sections - 1)
            def _():
                send(out.at[m, :, cut], xbuf.at[m, :, cut], 0, m, s + 1, d)

        pltpu.make_async_copy(out.at[m], out_hbm.at[m], store_sem.at[m]).start()

    def step_values(m):
        wait_in(sq.at[m, pl.ds(0, dp - 1)], 1, m)
        total_sq = jnp.sum(sq[m], axis=0)
        inv = lax.rsqrt(total_sq / model_width + 0.25)
        invs[...] = jnp.broadcast_to(inv[0:1, :], (rows_all, rows_all)).T
        wait_in(rs_recv.at[m], 3, m)
        total = csum[pl.ds(pl.multiple_of(z * rows, rows), rows), :]
        for j in range(chips - 1):
            total = total + rs_recv[m, j].astype(F32)
        own = invs[pl.ds(pl.multiple_of(c * half + z * rows, rows), rows), 0:1]
        vals[m, c, z] = (own * total).astype(BF16)
        for j in range(1, chips):
            target = lax.rem(z + j, chips)
            send(vals.at[m, c, z], vals.at[m, c, z], 4, m, s, target * 2 + c)

        @pl.when(m == 0)
        def _():
            loads[1].wait()

        weighted[m] = (invs[:, 0:1] * cot[m].astype(F32)).astype(BF16)

    contract_rows = (((0,), (0,)), ((), ()))
    tile = 256
    group = max(1, 256 // rows_all)
    groups = micro // group

    def gradient_tile(pair, n):
        at = pl.ds(pl.multiple_of(n * tile, tile), tile)
        left = scaled[pl.ds(pair * group, group), :, at].reshape(group * rows_all, tile)
        right = weighted[pl.ds(pair * group, group)].reshape(group * rows_all, width)
        return at, lax.dot_general(left, right, contract_rows, preferred_element_type=F32)

    def step_gradient(t):
        pair = (t - group) // group
        side = lax.rem(t, group)
        tiles = cols // tile // group

        @pl.loop(0, tiles)
        def _(i):
            at, update = gradient_tile(pair, side * tiles + i)

            @pl.when(pair == 0)
            def _():
                acc[at, :] = update

            @pl.when(pair > 0)
            def _():
                acc[at, :] += update

    def step_last_gradient():
        @pl.loop(0, cols // tile)
        def _(n):
            at, update = gradient_tile(groups - 1, n)
            grad[at, :] = (acc[at, :] + update).astype(BF16)

    def step_right():
        for j in [*range(1, chips), 0]:
            target = lax.rem(z + j, chips)
            at = pl.ds(pl.multiple_of(target * 2 * share, 2 * share), 2 * share)

            @pl.loop(0, width // 256)
            def _(n):
                cut = pl.ds(pl.multiple_of(n * 256, 256), 256)
                product = lax.dot_general(
                    grad[:, at], grad[:, cut], contract_rows, preferred_element_type=F32
                )
                right_own[j, 0, :, cut] = product[:share]
                right_own[j, 1, :, cut] = product[share:]

            right_send[j] = right_own[j, 1 - c].astype(BF16)
            pltpu.make_async_remote_copy(
                src_ref=right_send.at[j], dst_ref=right_recv.at[j],
                send_sem=right_sem.at[0, j], recv_sem=right_sem.at[1, j],
                device_id=device(s, partner), device_id_type=MESH,
            ).start()
        for j in [*range(1, chips), 0]:
            pltpu.make_async_copy(right_recv.at[j], right_recv.at[j], right_sem.at[1, j]).wait()
            parts[j][...] = (right_own[j, c] + right_recv[j].astype(F32)).astype(BF16)
        for j in range(chips):
            pltpu.make_async_copy(right_send.at[j], right_send.at[j], right_sem.at[0, j]).wait()

    @pl.loop(0, micro + 2)
    def _(t):
        @pl.when(t < micro)
        def _():
            step_project(t)

        @pl.when((t >= 1) & (t <= micro))
        def _():
            step_values(t - 1)

        @pl.when(t >= 2)
        def _():
            step_forward(t - 2)

        @pl.when(t < micro)
        def _():
            step_scatter(t)

        @pl.when(t >= 2)
        def _():
            step_output(t - 2)

        @pl.when((t >= group) & (t < micro))
        def _():
            step_gradient(t)

        @pl.when(t == micro)
        def _():
            step_last_gradient()

    step_right()

    @pl.loop(0, micro)
    def _(m):
        wait_out(sq.at[m, pl.ds(0, dp - 1)], 1, m)
        wait_out(pair_send.at[m], 2, m)
        wait_out(rs_send.at[m], 3, m)
        wait_out(vals.at[m, c, pl.ds(0, chips - 1)], 4, m)
        wait_out(vals.at[m, c], 5, m)
        pltpu.make_async_copy(out.at[m], out_hbm.at[m], store_sem.at[m]).wait()

        @pl.when(s < sections - 1)
        def _():
            wait_out(out.at[m], 0, m)


def relay(sections, dp, x_in, cot, gain, wv, wo):
    micro, rows_all, cols = x_in.shape
    width = wv.shape[1]
    chips = dp // 2
    half = rows_all // 2
    rows = half // chips
    share = width // dp
    vmem = pl.BlockSpec(memory_space=pltpu.VMEM)
    anywhere = pl.BlockSpec(memory_space=pl.ANY)
    return pl.pallas_call(
        functools.partial(relay_kernel, sections, dp, cols * dp),
        out_shape=(
            jax.ShapeDtypeStruct((micro, rows_all, cols), BF16),
            jax.ShapeDtypeStruct((cols, width), BF16),
            *[jax.ShapeDtypeStruct((share, width), BF16)] * chips,
        ),
        in_specs=[anywhere, anywhere, vmem, anywhere, anywhere],
        out_specs=(anywhere, vmem, *[vmem] * chips),
        scratch_shapes=[
            pltpu.VMEM((micro, rows_all, cols), BF16),
            pltpu.VMEM((micro, rows_all, cols), BF16),
            pltpu.VMEM((micro, rows_all, width), BF16),
            pltpu.VMEM((micro, rows_all, width), BF16),
            pltpu.VMEM((cols, width), BF16),
            pltpu.VMEM((width, cols), BF16),
            pltpu.VMEM((cols, width), F32),
            pltpu.VMEM((chips, 2, share, width), F32),
            pltpu.VMEM((chips, share, width), BF16),
            pltpu.VMEM((chips, share, width), BF16),
            pltpu.VMEM((micro, rows_all, cols), BF16),
            pltpu.VMEM((rows_all, width), F32),
            pltpu.VMEM((half, width), F32),
            pltpu.VMEM((rows_all, rows_all), F32),
            pltpu.VMEM((micro, dp, 8, rows_all), F32),
            pltpu.VMEM((micro, half, width), BF16),
            pltpu.VMEM((micro, half, width), BF16),
            pltpu.VMEM((micro, chips - 1, rows, width), BF16),
            pltpu.VMEM((micro, chips - 1, rows, width), BF16),
            pltpu.VMEM((micro, 2, chips, rows, width), BF16),
            pltpu.SemaphoreType.DMA((6, micro)),
            pltpu.SemaphoreType.DMA((6, micro)),
            pltpu.SemaphoreType.DMA((3,)),
            pltpu.SemaphoreType.DMA((micro,)),
            pltpu.SemaphoreType.DMA((2, chips)),
        ],
        compiler_params=pltpu.CompilerParams(
            collective_id=0, has_side_effects=True, vmem_limit_bytes=58 * 1024 * 1024
        ),
    )(x_in, cot, gain, wv, wo)


def on_device(inputs, cotangent, norm_gain, value_weight, output_weight, left_old, right_old):
    sections = lax.axis_size("section")
    dp = lax.axis_size("dp")
    micro, rows_all, cols = inputs.shape
    width = value_weight.shape[2]
    chips = dp // 2
    split = 2 if rows_all // dp >= 16 else 1
    chunked = (micro * split, rows_all // split)
    outputs, grad_half, *parts = relay(
        sections, dp, inputs.reshape(chunked + (cols,)), cotangent[0].reshape(chunked + (width,)),
        norm_gain, value_weight[0], output_weight[0]
    )
    outputs = outputs.reshape(micro, rows_all, cols)
    moved = [
        lax.ppermute(
            parts[j], "dp",
            [(z * 2 + c, (z + j) % chips * 2 + c) for z in range(chips) for c in range(2)],
        )
        for j in range(1, chips)
    ]
    blocks = grad_half.reshape(cols // BLOCK, BLOCK, width)
    left_new = (
        left_old[0] + jnp.einsum("bik,bjk->bij", blocks, blocks, preferred_element_type=F32) / BLOCK
    )
    right_rows = parts[0].astype(F32)
    for piece in moved:
        right_rows = right_rows + piece.astype(F32)
    right_new = right_old[0] + right_rows / (cols * dp)
    return (outputs[None], left_new[None], right_new[None])


def solution(mesh):
    placed = (
        P(None, None, "dp"),
        P("section", None, None, None),
        P("section", "dp"),
        P("section", "dp", None),
        P("section", None, "dp"),
        P("section", "dp", None, None),
        P("section", "dp", None),
    )
    return jax.shard_map(
        on_device,
        mesh=mesh,
        in_specs=placed,
        out_specs=(
            P("section", None, None, "dp"),
            P("section", "dp", None, None),
            P("section", "dp", None),
        ),
        check_vma=False,
    )
```

profile of v0, /device:TPU:15, one launch (start us, length us, event | category | flops | bytes accessed | tf_op | source)
XLA Modules:
  0.0 213.5 jit_solution(1883562385557068255)
XLA Ops:
  0.6 183.5 %shard_map.94 = (bf16[16,64,2048]{2,1,0:T(8,128)(2,1)}, bf16[2048,1024]{1,0:T(8,128)(2,1)}, bf16[128,1024]{1,0:T(8,128)(2,1)}, bf16[128,1024]{1,0:T(8,128)(2,1)}...) custom-call(bf16[16,64,2048]{2,1,0:T(8,128)(2,1)} %bitcast.20, bf16[16,64,1024]{2,1,0:T(8,128)(2,1)} %bitcast.24, ...), custom_call_target="tpu_custom_call" | custom-call | tf_op jit(solution)/shard_map/pallas_call | solution.py:290
  184.2 0.8 collective-permute-start
  185.0 2.1 %collective-permute-start.1 = (bf16[128,1024]{1,0:T(8,128)(2,1)}, bf16[128,1024]{1,0:T(8,128)(2,1)S(1)}, u32[]{:S(2)}, u32[]{:S(2)}) collective-permute-start(bf16[128,1024]{1,0:T(8,128)(2,1)} %get-tuple-element.13), channel_id=1, source_target_pairs={{0,4},{1,5},{2,6},{3,7},{4,0},{5,1},{6,2},{7,3},{8,12},{9,13},{10,... | collective-permute-start | bytes 786440 | tf_op jit(solution)/shard_map/ppermute | solution.py:346
  187.1 0.6 collective-permute-start.2
  187.7 0.0 copy-start.1
  187.7 0.0 copy-start.2
  187.7 0.0 copy-start
  187.7 13.9 %fusion = f32[1,2,1024,1024]{3,2,1,0:T(8,128)} fusion(f32[1,2,1024,1024]{3,2,1,0:T(8,128)} %param.12, bf16[2,1024,1024]{2,1,0:T(8,128)(2,1)} %bitcast.25), kind=kOutput, calls=%fused_computation.1 | convolution fusion | flops 4299161600 | bytes 20971520 | tf_op jit(solution)/shard_map/bik,bjk->bij/dot_general | solution.py:354
  201.7 0.0 collective-permute-done
  201.7 6.1 %collective-permute-done.1 = bf16[128,1024]{1,0:T(8,128)(2,1)S(1)} collective-permute-done((bf16[128,1024]{1,0:T(8,128)(2,1)}, bf16[128,1024]{1,0:T(8,128)(2,1)S(1)}, u32[]{:S(2)}, u32[]{:S(2)}) %collective-permute-start.1) | collective-permute-done | bytes 262176 | tf_op jit(solution)/shard_map/ppermute | solution.py:346
  207.7 2.7 %collective-permute-done.2 = bf16[128,1024]{1,0:T(8,128)(2,1)S(1)} collective-permute-done((bf16[128,1024]{1,0:T(8,128)(2,1)}, bf16[128,1024]{1,0:T(8,128)(2,1)S(1)}, u32[]{:S(2)}, u32[]{:S(2)}) %collective-permute-start.2) | collective-permute-done | bytes 262176 | tf_op jit(solution)/shard_map/ppermute | solution.py:346
  210.4 0.0 copy-done.1
  210.5 0.0 copy-done.2
  210.5 1.0 fusion.1
  211.4 0.0 copy-done
  211.4 2.0 copy.11
Async XLA Ops:
  184.2 17.5 %collective-permute-start = (bf16[128,1024]{1,0:T(8,128)(2,1)}, bf16[128,1024]{1,0:T(8,128)(2,1)S(1)}, u32[]{:S(2)}, u32[]{:S(2)}) collective-permute-start(bf16[128,1024]{1,0:T(8,128)(2,1)} %get-tuple-element.12), channel_id=1, source_target_pairs={{0,2},{1,3},{2,4},{3,5},{4,6},{5,7},{6,0},{7,1},{8,10},{9,11},{10,... | collective-permute-start | bytes 786440 | tf_op jit(solution)/shard_map/ppermute | solution.py:346
  185.0 22.7 %collective-permute-start.1 = (bf16[128,1024]{1,0:T(8,128)(2,1)}, bf16[128,1024]{1,0:T(8,128)(2,1)S(1)}, u32[]{:S(2)}, u32[]{:S(2)}) collective-permute-start(bf16[128,1024]{1,0:T(8,128)(2,1)} %get-tuple-element.13), channel_id=1, source_target_pairs={{0,4},{1,5},{2,6},{3,7},{4,0},{5,1},{6,2},{7,3},{8,12},{9,13},{10,... | collective-permute-start | bytes 786440 | tf_op jit(solution)/shard_map/ppermute | solution.py:346
  187.1 23.3 %collective-permute-start.2 = (bf16[128,1024]{1,0:T(8,128)(2,1)}, bf16[128,1024]{1,0:T(8,128)(2,1)S(1)}, u32[]{:S(2)}, u32[]{:S(2)}) collective-permute-start(bf16[128,1024]{1,0:T(8,128)(2,1)} %get-tuple-element.14), channel_id=1, source_target_pairs={{0,6},{1,7},{2,0},{3,1},{4,2},{5,3},{6,4},{7,5},{8,14},{9,15},{10,... | collective-permute-start | bytes 786440 | tf_op jit(solution)/shard_map/ppermute | solution.py:346
  187.7 22.7 %copy-start.1 = (f32[1,128,1024]{2,1,0:T(8,128)S(1)}, f32[1,128,1024]{2,1,0:T(8,128)}, u32[]{:S(2)}) copy-start(f32[1,128,1024]{2,1,0:T(8,128)} %param.13) | copy-start | bytes 1572868
  187.7 22.7 %copy-start.2 = (bf16[128,1024]{1,0:T(8,128)(2,1)S(1)}, bf16[128,1024]{1,0:T(8,128)(2,1)}, u32[]{:S(2)}) copy-start(bf16[128,1024]{1,0:T(8,128)(2,1)} %get-tuple-element.11) | copy-start | bytes 786436
  187.7 23.7 %copy-start = (bf16[16,64,2048]{2,1,0:T(8,128)(2,1)S(1)}, bf16[16,64,2048]{2,1,0:T(8,128)(2,1)}, u32[]{:S(2)}) copy-start(bf16[16,64,2048]{2,1,0:T(8,128)(2,1)} %get-tuple-element.9) | copy-start | bytes 12582916
where the time goes:
time: 214 us; the launch traced here: 213 us
  Pallas kernels  184 us (86%)
  matrix products  13.9 us (6%)
  waiting for transfers between devices  8.79 us (4%)
  starting transfers between devices  3.57 us (2%)
    pallas_call x1, Pallas kernels, relay(): pl.pallas_call(functools.partial(relay_kernel, sections, dp, cols * dp),...  184 us
    dot_general x1, matrix products, on_device(): jnp.einsum('bik,bjk->bij', blocks, blocks, preferred_element_type=F32)  13.9 us
    ppermute x3, waiting for transfers between devices, on_device(): lax.ppermute(parts[j], 'dp', [(z * 2 + c, (z + j) % chips * 2 + c) for z...  8.79 us
  transfers between devices with their start and end apart: 3, of which 2 were waited for; matrix products, arithmetic and copies ran while one was open for 7% of the time, Pallas kernels for 0%

commit v1 on v0

--- a/solution.py
+++ b/solution.py
@@ -8,6 +8,7 @@
 from jax.sharding import PartitionSpec as P
 
 BLOCK = 1024
+VMEM_BYTES = 46 * 1024 * 1024
 MESH = pl.DeviceIdType.MESH
 F32 = jnp.float32
 BF16 = jnp.bfloat16
@@ -15,17 +16,14 @@
 
 def relay_kernel(
     sections, dp, model_width,
-    x_in, cot_in, gain, wv_in, wo_in,
-    *refs,
+    x_in, cot_in, gain, wv_in, wo_in, left_in, right_in,
+    out, acc, right_out,
+    grad, scaled, weighted, cot, wv, wo, right_own, right_send, right_recv,
+    z_send, z_recv,
+    xbuf, prod, csum, invs, sq, pair_send, pair_recv, rs_send, rs_recv, vals,
+    send_sem, recv_sem, load_sem, right_sem, z_sem,
 ):
     chips = dp // 2
-    out_hbm, grad = refs[:2]
-    parts = refs[2:2 + chips]
-    (
-        out, scaled, weighted, cot, wv, wo, acc, right_own, right_send, right_recv,
-        xbuf, prod, csum, invs, sq, pair_send, pair_recv, rs_send, rs_recv, vals,
-        send_sem, recv_sem, load_sem, store_sem, right_sem,
-    ) = refs[2 + chips:]
     micro, rows_all, cols = x_in.shape
     width = wv.shape[1]
     half = rows_all // 2
@@ -42,8 +40,9 @@
 
     loads = [
         pltpu.make_async_copy(src, dst, load_sem.at[i])
-        for i, (src, dst) in enumerate(((wv_in, wv), (cot_in, cot), (wo_in, wo)))
+        for i, (src, dst) in enumerate(((wv_in, wv), (cot_in, cot), (wo_in, wo), (right_in, right_out)))
     ]
+    left_load = pltpu.make_async_copy(left_in, acc, load_sem.at[4])
 
     @pl.when(s == 0)
     def _():
@@ -148,8 +147,6 @@
             @pl.when(s < sections - 1)
             def _():
                 send(out.at[m, :, cut], xbuf.at[m, :, cut], 0, m, s + 1, d)
-
-        pltpu.make_async_copy(out.at[m], out_hbm.at[m], store_sem.at[m]).start()
 
     def step_values(m):
         wait_in(sq.at[m, pl.ds(0, dp - 1)], 1, m)
@@ -206,31 +203,67 @@
             at, update = gradient_tile(groups - 1, n)
             grad[at, :] = (acc[at, :] + update).astype(BF16)
 
+    def right_product(j):
+        target = lax.rem(z + j, chips)
+        at = pl.ds(pl.multiple_of(target * 2 * share, 2 * share), 2 * share)
+
+        @pl.loop(0, width // 256)
+        def _(n):
+            cut = pl.ds(pl.multiple_of(n * 256, 256), 256)
+            product = lax.dot_general(
+                grad[:, at], grad[:, cut], contract_rows, preferred_element_type=F32
+            )
+            right_own[j, 0, :, cut] = product[:share]
+            right_own[j, 1, :, cut] = product[share:]
+
+        right_send[j] = right_own[j, 1 - c].astype(BF16)
+        pltpu.make_async_remote_copy(
+            src_ref=right_send.at[j], dst_ref=right_recv.at[j],
+            send_sem=right_sem.at[0, j], recv_sem=right_sem.at[1, j],
+            device_id=device(s, partner), device_id_type=MESH,
+        ).start()
+
+    def right_scatter(j):
+        pltpu.make_async_copy(right_recv.at[j], right_recv.at[j], right_sem.at[1, j]).wait()
+        z_send[j - 1] = (right_own[j, c] + right_recv[j].astype(F32)).astype(BF16)
+        pltpu.make_async_remote_copy(
+            src_ref=z_send.at[j - 1], dst_ref=z_recv.at[chips - 1 - j],
+            send_sem=z_sem.at[0, j - 1], recv_sem=z_sem.at[1, chips - 1 - j],
+            device_id=device(s, lax.rem(z + j, chips) * 2 + c), device_id_type=MESH,
+        ).start()
+
     def step_right():
-        for j in [*range(1, chips), 0]:
-            target = lax.rem(z + j, chips)
-            at = pl.ds(pl.multiple_of(target * 2 * share, 2 * share), 2 * share)
-
-            @pl.loop(0, width // 256)
+        for j in range(1, chips):
+            right_product(j)
+            if j > 1:
+                right_scatter(j - 1)
+        right_product(0)
+        right_scatter(chips - 1)
+
+    def step_left():
+        left_load.wait()
+        for block in range(cols // BLOCK):
+            @pl.loop(0, BLOCK // 256)
             def _(n):
-                cut = pl.ds(pl.multiple_of(n * 256, 256), 256)
+                at = pl.ds(pl.multiple_of(block * BLOCK + n * 256, 256), 256)
                 product = lax.dot_general(
-                    grad[:, at], grad[:, cut], contract_rows, preferred_element_type=F32
+                    grad[at, :], grad[block * BLOCK:(block + 1) * BLOCK, :],
+                    (((1,), (1,)), ((), ())), preferred_element_type=F32,
                 )
-                right_own[j, 0, :, cut] = product[:share]
-                right_own[j, 1, :, cut] = product[share:]
-
-            right_send[j] = right_own[j, 1 - c].astype(BF16)
-            pltpu.make_async_remote_copy(
-                src_ref=right_send.at[j], dst_ref=right_recv.at[j],
-                send_sem=right_sem.at[0, j], recv_sem=right_sem.at[1, j],
-                device_id=device(s, partner), device_id_type=MESH,
-            ).start()
-        for j in [*range(1, chips), 0]:
-            pltpu.make_async_copy(right_recv.at[j], right_recv.at[j], right_sem.at[1, j]).wait()
-            parts[j][...] = (right_own[j, c] + right_recv[j].astype(F32)).astype(BF16)
+                acc[at, :] += product * (1.0 / BLOCK)
+
+    def step_last_right():
+        pltpu.make_async_copy(right_recv.at[0], right_recv.at[0], right_sem.at[1, 0]).wait()
+        total = right_own[0, c] + right_recv[0].astype(F32)
+        for j in range(chips - 1):
+            pltpu.make_async_copy(z_recv.at[j], z_recv.at[j], z_sem.at[1, j]).wait()
+            total = total + z_recv[j].astype(F32)
+        loads[3].wait()
+        right_out[...] += total * (1.0 / model_width)
         for j in range(chips):
             pltpu.make_async_copy(right_send.at[j], right_send.at[j], right_sem.at[0, j]).wait()
+        for j in range(chips - 1):
+            pltpu.make_async_copy(z_send.at[j], z_send.at[j], z_sem.at[0, j]).wait()
 
     @pl.loop(0, micro + 2)
     def _(t):
@@ -244,25 +277,28 @@
 
         @pl.when(t >= 2)
         def _():
-            step_forward(t - 2)
+            step_output(t - 2)
 
         @pl.when(t < micro)
         def _():
             step_scatter(t)
 
-        @pl.when(t >= 2)
-        def _():
-            step_output(t - 2)
-
         @pl.when((t >= group) & (t < micro))
         def _():
             step_gradient(t)
 
+        @pl.when((t >= 1) & (t <= micro))
+        def _():
+            step_forward(t - 1)
+
         @pl.when(t == micro)
         def _():
             step_last_gradient()
 
+    left_load.start()
     step_right()
+    step_left()
+    step_last_right()
 
     @pl.loop(0, micro)
     def _(m):
@@ -271,14 +307,13 @@
         wait_out(rs_send.at[m], 3, m)
         wait_out(vals.at[m, c, pl.ds(0, chips - 1)], 4, m)
         wait_out(vals.at[m, c], 5, m)
-        pltpu.make_async_copy(out.at[m], out_hbm.at[m], store_sem.at[m]).wait()
 
         @pl.when(s < sections - 1)
         def _():
             wait_out(out.at[m], 0, m)
 
 
-def relay(sections, dp, x_in, cot, gain, wv, wo):
+def relay(sections, dp, x_in, cot, gain, wv, wo, left, right):
     micro, rows_all, cols = x_in.shape
     width = wv.shape[1]
     chips = dp // 2
@@ -290,23 +325,24 @@
     return pl.pallas_call(
         functools.partial(relay_kernel, sections, dp, cols * dp),
         out_shape=(
-            jax.ShapeDtypeStruct((micro, rows_all, cols), BF16),
-            jax.ShapeDtypeStruct((cols, width), BF16),
-            *[jax.ShapeDtypeStruct((share, width), BF16)] * chips,
+            pltpu.VMEM((micro, rows_all, cols), BF16),
+            pltpu.VMEM((cols, width), F32),
+            pltpu.VMEM((share, width), F32),
         ),
-        in_specs=[anywhere, anywhere, vmem, anywhere, anywhere],
-        out_specs=(anywhere, vmem, *[vmem] * chips),
+        in_specs=[anywhere, anywhere, vmem, anywhere, anywhere, anywhere, anywhere],
+        out_specs=(vmem, vmem, vmem),
         scratch_shapes=[
-            pltpu.VMEM((micro, rows_all, cols), BF16),
+            pltpu.VMEM((cols, width), BF16),
             pltpu.VMEM((micro, rows_all, cols), BF16),
             pltpu.VMEM((micro, rows_all, width), BF16),
             pltpu.VMEM((micro, rows_all, width), BF16),
             pltpu.VMEM((cols, width), BF16),
             pltpu.VMEM((width, cols), BF16),
-            pltpu.VMEM((cols, width), F32),
             pltpu.VMEM((chips, 2, share, width), F32),
             pltpu.VMEM((chips, share, width), BF16),
             pltpu.VMEM((chips, share, width), BF16),
+            pltpu.VMEM((chips - 1, share, width), BF16),
+            pltpu.VMEM((chips - 1, share, width), BF16),
             pltpu.VMEM((micro, rows_all, cols), BF16),
             pltpu.VMEM((rows_all, width), F32),
             pltpu.VMEM((half, width), F32),
@@ -319,14 +355,14 @@
             pltpu.VMEM((micro, 2, chips, rows, width), BF16),
             pltpu.SemaphoreType.DMA((6, micro)),
             pltpu.SemaphoreType.DMA((6, micro)),
-            pltpu.SemaphoreType.DMA((3,)),
-            pltpu.SemaphoreType.DMA((micro,)),
+            pltpu.SemaphoreType.DMA((5,)),
             pltpu.SemaphoreType.DMA((2, chips)),
+            pltpu.SemaphoreType.DMA((2, chips - 1)),
         ],
         compiler_params=pltpu.CompilerParams(
-            collective_id=0, has_side_effects=True, vmem_limit_bytes=58 * 1024 * 1024
+            collective_id=0, has_side_effects=True, vmem_limit_bytes=VMEM_BYTES
         ),
-    )(x_in, cot, gain, wv, wo)
+    )(x_in, cot, gain, wv, wo, left, right)
 
 
 def on_device(inputs, cotangent, norm_gain, value_weight, output_weight, left_old, right_old):
@@ -337,27 +373,12 @@
     chips = dp // 2
     split = 2 if rows_all // dp >= 16 else 1
     chunked = (micro * split, rows_all // split)
-    outputs, grad_half, *parts = relay(
+    outputs, left_new, right_new = relay(
         sections, dp, inputs.reshape(chunked + (cols,)), cotangent[0].reshape(chunked + (width,)),
-        norm_gain, value_weight[0], output_weight[0]
+        norm_gain, value_weight[0], output_weight[0], left_old.reshape(cols, width), right_old[0],
     )
-    outputs = outputs.reshape(micro, rows_all, cols)
-    moved = [
-        lax.ppermute(
-            parts[j], "dp",
-            [(z * 2 + c, (z + j) % chips * 2 + c) for z in range(chips) for c in range(2)],
-        )
-        for j in range(1, chips)
-    ]
-    blocks = grad_half.reshape(cols // BLOCK, BLOCK, width)
-    left_new = (
-        left_old[0] + jnp.einsum("bik,bjk->bij", blocks, blocks, preferred_element_type=F32) / BLOCK
-    )
-    right_rows = parts[0].astype(F32)
-    for piece in moved:
-        right_rows = right_rows + piece.astype(F32)
-    right_new = right_old[0] + right_rows / (cols * dp)
-    return (outputs[None], left_new[None], right_new[None])
+    outputs = outputs.reshape((1, micro, rows_all, cols))
+    return (outputs, left_new.reshape(left_old.shape), right_new[None])
 
 
 def solution(mesh):

time: 214 us -> 206 us (0.963)
  Pallas kernels: 184 us -> 199 us
  matrix products: 13.9 us -> 0 us
  waiting for transfers between devices: 8.79 us -> 0 us
  local copies, waits for them, and re-layouts: 2.02 us -> 6.2 us
  starting transfers between devices: 3.57 us -> 0 us
    pallas_call x1, Pallas kernels: 184 us -> 199 us  [relay(): pl.pallas_call(functools.partial(relay_kernel, sections, dp, cols * dp),...]
    dot_general x1 -> x0, matrix products: 13.9 us -> none  [on_device(): jnp.einsum('bik,bjk->bij', blocks, blocks, preferred_element_type=F32)]
    ppermute x3 -> x0, waiting for transfers between devices: 8.79 us -> none  [on_device(): lax.ppermute(parts[j], 'dp', [(z * 2 + c, (z + j) % chips * 2 + c) for z...]
    unnamed x7 -> x3, local copies, waits for them, and re-layouts: 2.02 us -> 6.2 us
    ppermute x3 -> x0, starting transfers between devices: 3.57 us -> none  [on_device(): lax.ppermute(parts[j], 'dp', [(z * 2 + c, (z + j) % chips * 2 + c) for z...]
  transfers between devices with their start and end apart: 3 -> 0, of which waited for: 2 -> 0; matrix products, arithmetic and copies ran while one was open for 7% -> 0% of each run, Pallas kernels for 0% -> 0%
where the time goes in v1:
time: 206 us
  Pallas kernels  199 us (97%)
  local copies, waits for them, and re-layouts  6.2 us (3%)
    pallas_call x1, Pallas kernels, relay(): pl.pallas_call(functools.partial(relay_kernel, sections, dp, cols * dp),...  199 us
    unnamed x3, local copies, waits for them, and re-layouts  6.2 us

profile of v1, /device:TPU:15, one launch (start us, length us, event | category | flops | bytes accessed | tf_op | source)
XLA Modules:
  0.0 205.6 jit_solution(16240578010941248750)
XLA Ops:
  0.6 198.8 %shard_map.94 = (bf16[16,64,2048]{2,1,0:T(8,128)(2,1)S(1)}, f32[2048,1024]{1,0:T(8,128)S(1)}, f32[128,1024]{1,0:T(8,128)S(1)}) custom-call(bf16[16,64,2048]{2,1,0:T(8,128)(2,1)} %bitcast.13, bf16[16,64,1024]{2,1,0:T(8,128)(2,1)} %bitcast.16, bf16[1,2048]{1,0:T(2,128)(2,1)} %gain.1, bf16[2048,1024]{1,0:T(8,128)(2,1)} %bitcast.14, ...), custom_call_target="tpu_custom_call" | custom-call | tf_op jit(solution)/shard_map/pallas_call | solution.py:325
  199.4 2.0 copy.13
  201.4 3.4 %copy.14 = f32[1,2,1024,1024]{3,2,1,0:T(8,128)} copy(f32[1,2,1024,1024]{3,2,1,0:T(8,128)S(1)} %bitcast.9) | data formatting | bytes 16777216
  204.8 0.8 copy.15

commit v2 on v1

--- a/solution.py
+++ b/solution.py
@@ -19,9 +19,9 @@
     x_in, cot_in, gain, wv_in, wo_in, left_in, right_in,
     out, acc, right_out,
     grad, scaled, weighted, cot, wv, wo, right_own, right_send, right_recv,
-    z_send, z_recv,
+    z_send, z_recv, help_in, help_recv, help_send, help_back,
     xbuf, prod, csum, invs, sq, pair_send, pair_recv, rs_send, rs_recv, vals,
-    send_sem, recv_sem, load_sem, right_sem, z_sem,
+    send_sem, recv_sem, load_sem, right_sem, z_sem, help_sem, back_sem,
 ):
     chips = dp // 2
     micro, rows_all, cols = x_in.shape
@@ -34,6 +34,10 @@
     z = d // 2
     c = lax.rem(d, 2)
     partner = z * 2 + (1 - c)
+    last = sections - 1
+    helpers = (last ^ 2, last ^ 3) if sections % 4 == 0 else ()
+    own_cols = width // 2 if helpers else width
+    slice_cols = (width - own_cols) // max(1, len(helpers))
 
     def device(section, index):
         return (section, index)
@@ -48,8 +52,7 @@
     def _():
         pltpu.make_async_copy(x_in.at[0], xbuf.at[0], recv_sem.at[0, 0]).start()
 
-    for load in loads:
-        load.start()
+    loads[0].start()
 
     @pl.when(s == 0)
     def _():
@@ -69,9 +72,15 @@
     def _():
         pl.semaphore_signal(barrier, inc=1, device_id=device(s + 1, d), device_id_type=MESH)
 
-    pl.semaphore_wait(
-        barrier, dp - 1 + jnp.minimum(s, 1) + jnp.minimum(sections - 1 - s, 1)
-    )
+    greeted = dp - 1 + jnp.minimum(s, 1) + jnp.minimum(sections - 1 - s, 1)
+    for h in helpers:
+        for there, here in ((last, h), (h, last)):
+            @pl.when(s == here)
+            def _():
+                pl.semaphore_signal(barrier, inc=1, device_id=device(there, d), device_id_type=MESH)
+
+            greeted = greeted + jnp.where(s == here, 1, 0)
+    pl.semaphore_wait(barrier, greeted)
 
     def send(src, dst, phase, m, section, index):
         pltpu.make_async_remote_copy(
@@ -103,11 +112,10 @@
         @pl.when(m == 0)
         def _():
             loads[0].wait()
-
-        @pl.loop(0, width // 256)
-        def _(n):
-            at = pl.ds(pl.multiple_of(n * 256, 256), 256)
-            prod[:, at] = jnp.dot(scaled[m], wv[:, at], preferred_element_type=F32)
+            for load in loads[1:]:
+                load.start()
+
+        prod[...] = jnp.dot(scaled[m], wv[...], preferred_element_type=F32)
 
         pair_send[m] = prod[pl.ds(pl.multiple_of((1 - c) * half, half), half), :].astype(BF16)
         send(pair_send.at[m], pair_recv.at[m], 2, m, s, partner)
@@ -133,26 +141,34 @@
 
         values = vals[m].reshape(rows_all, width)
 
-        for side in range(2):
-            @pl.loop(0, cols // 1024)
+        for side in range(4):
+            @pl.loop(0, cols // 2048)
             def _(n):
-                at = pl.ds(pl.multiple_of(side * (cols // 2) + n * 512, 512), 512)
+                at = pl.ds(pl.multiple_of(side * (cols // 4) + n * 512, 512), 512)
                 out[m, :, at] = (
                     xbuf[m, :, at].astype(F32)
                     + jnp.dot(values, wo[:, at], preferred_element_type=F32)
                 ).astype(BF16)
 
-            cut = pl.ds(side * (cols // 2), cols // 2)
+            cut = pl.ds(side * (cols // 4), cols // 4)
 
             @pl.when(s < sections - 1)
             def _():
                 send(out.at[m, :, cut], xbuf.at[m, :, cut], 0, m, s + 1, d)
 
-    def step_values(m):
+    def step_weigh(m):
         wait_in(sq.at[m, pl.ds(0, dp - 1)], 1, m)
         total_sq = jnp.sum(sq[m], axis=0)
         inv = lax.rsqrt(total_sq / model_width + 0.25)
         invs[...] = jnp.broadcast_to(inv[0:1, :], (rows_all, rows_all)).T
+
+        @pl.when(m == 0)
+        def _():
+            loads[1].wait()
+
+        weighted[m] = (invs[:, 0:1] * cot[m].astype(F32)).astype(BF16)
+
+    def step_values(m):
         wait_in(rs_recv.at[m], 3, m)
         total = csum[pl.ds(pl.multiple_of(z * rows, rows), rows), :]
         for j in range(chips - 1):
@@ -163,12 +179,6 @@
             target = lax.rem(z + j, chips)
             send(vals.at[m, c, z], vals.at[m, c, z], 4, m, s, target * 2 + c)
 
-        @pl.when(m == 0)
-        def _():
-            loads[1].wait()
-
-        weighted[m] = (invs[:, 0:1] * cot[m].astype(F32)).astype(BF16)
-
     contract_rows = (((0,), (0,)), ((), ()))
     tile = 256
     group = max(1, 256 // rows_all)
@@ -207,15 +217,10 @@
         target = lax.rem(z + j, chips)
         at = pl.ds(pl.multiple_of(target * 2 * share, 2 * share), 2 * share)
 
-        @pl.loop(0, width // 256)
-        def _(n):
-            cut = pl.ds(pl.multiple_of(n * 256, 256), 256)
-            product = lax.dot_general(
-                grad[:, at], grad[:, cut], contract_rows, preferred_element_type=F32
-            )
-            right_own[j, 0, :, cut] = product[:share]
-            right_own[j, 1, :, cut] = product[share:]
-
+        product = lax.dot_general(
+            grad[:, at], grad[...], contract_rows, preferred_element_type=F32
+        )
+        right_own[j] = product.reshape(2, share, width)
         right_send[j] = right_own[j, 1 - c].astype(BF16)
         pltpu.make_async_remote_copy(
             src_ref=right_send.at[j], dst_ref=right_recv.at[j],
@@ -226,11 +231,28 @@
     def right_scatter(j):
         pltpu.make_async_copy(right_recv.at[j], right_recv.at[j], right_sem.at[1, j]).wait()
         z_send[j - 1] = (right_own[j, c] + right_recv[j].astype(F32)).astype(BF16)
-        pltpu.make_async_remote_copy(
-            src_ref=z_send.at[j - 1], dst_ref=z_recv.at[chips - 1 - j],
-            send_sem=z_sem.at[0, j - 1], recv_sem=z_sem.at[1, chips - 1 - j],
-            device_id=device(s, lax.rem(z + j, chips) * 2 + c), device_id_type=MESH,
-        ).start()
+        target = lax.rem(z + j, chips) * 2 + c
+        slot = chips - 1 - j
+
+        def scatter(cut, dst, part, recv, section, target=target):
+            pltpu.make_async_remote_copy(
+                src_ref=z_send.at[j - 1, :, cut], dst_ref=dst,
+                send_sem=z_sem.at[0, j - 1, part], recv_sem=recv,
+                device_id=device(section, target), device_id_type=MESH,
+            ).start()
+
+        own = pl.ds(0, own_cols)
+        scatter(own, z_recv.at[slot, :, own], 0, z_sem.at[1, slot, 0], s)
+        for i, h in enumerate(helpers):
+            cut = pl.ds(own_cols + i * slice_cols, slice_cols)
+
+            @pl.when(s == last)
+            def _():
+                scatter(cut, help_in.at[j - 1], 1 + i, help_sem.at[0, j - 1], h, d)
+
+            @pl.when(s < last)
+            def _():
+                scatter(cut, z_recv.at[slot, :, cut], 1 + i, z_sem.at[1, slot, 1 + i], s)
 
     def step_right():
         for j in range(1, chips):
@@ -254,51 +276,189 @@
 
     def step_last_right():
         pltpu.make_async_copy(right_recv.at[0], right_recv.at[0], right_sem.at[1, 0]).wait()
-        total = right_own[0, c] + right_recv[0].astype(F32)
-        for j in range(chips - 1):
-            pltpu.make_async_copy(z_recv.at[j], z_recv.at[j], z_sem.at[1, j]).wait()
-            total = total + z_recv[j].astype(F32)
         loads[3].wait()
-        right_out[...] += total * (1.0 / model_width)
+        scale = 1.0 / model_width
+
+        def gather(cut, part):
+            total = right_own[0, c, :, cut] + right_recv[0, :, cut].astype(F32)
+            for k in range(chips - 1):
+                ref = z_recv.at[k, :, cut]
+                pltpu.make_async_copy(ref, ref, z_sem.at[1, k, part]).wait()
+                total = total + z_recv[k, :, cut].astype(F32)
+            right_out[:, cut] += total * scale
+
+        gather(pl.ds(0, own_cols), 0)
+        for i, h in enumerate(helpers):
+            cut = pl.ds(own_cols + i * slice_cols, slice_cols)
+
+            @pl.when(s == last)
+            def _():
+                ref = help_back.at[i]
+                pltpu.make_async_copy(ref, ref, back_sem.at[1, i]).wait()
+                total = right_own[0, c, :, cut] + right_recv[0, :, cut].astype(F32)
+                right_out[:, cut] += (total + help_back[i].astype(F32)) * scale
+
+            @pl.when(s < last)
+            def _():
+                gather(cut, 1 + i)
+
         for j in range(chips):
             pltpu.make_async_copy(right_send.at[j], right_send.at[j], right_sem.at[0, j]).wait()
         for j in range(chips - 1):
-            pltpu.make_async_copy(z_send.at[j], z_send.at[j], z_sem.at[0, j]).wait()
-
-    @pl.loop(0, micro + 2)
-    def _(t):
-        @pl.when(t < micro)
-        def _():
-            step_project(t)
-
-        @pl.when((t >= 1) & (t <= micro))
-        def _():
-            step_values(t - 1)
-
-        @pl.when(t >= 2)
-        def _():
-            step_output(t - 2)
-
-        @pl.when(t < micro)
-        def _():
-            step_scatter(t)
-
-        @pl.when((t >= group) & (t < micro))
-        def _():
-            step_gradient(t)
-
-        @pl.when((t >= 1) & (t <= micro))
-        def _():
-            step_forward(t - 1)
-
-        @pl.when(t == micro)
-        def _():
-            step_last_gradient()
-
-    left_load.start()
-    step_right()
+            for part in range(1 + len(helpers)):
+                ref = z_send.at[j, :, pl.ds(0, slice_cols if part else own_cols)]
+                pltpu.make_async_copy(ref, ref, z_sem.at[0, j, part]).wait()
+
+    def step_help():
+        for i, h in enumerate(helpers):
+            @pl.when(s == h)
+            def _():
+                for j in range(1, chips):
+                    ref = help_in.at[j - 1]
+                    pltpu.make_async_copy(ref, ref, help_sem.at[0, j - 1]).wait()
+                    pltpu.make_async_remote_copy(
+                        src_ref=ref, dst_ref=help_recv.at[chips - 1 - j],
+                        send_sem=help_sem.at[2, j - 1], recv_sem=help_sem.at[1, chips - 1 - j],
+                        device_id=device(s, lax.rem(z + j, chips) * 2 + c), device_id_type=MESH,
+                    ).start()
+                total = None
+                for k in range(chips - 1):
+                    ref = help_recv.at[k]
+                    pltpu.make_async_copy(ref, ref, help_sem.at[1, k]).wait()
+                    piece = help_recv[k].astype(F32)
+                    total = piece if total is None else total + piece
+                help_send[...] = total.astype(BF16)
+                back = pltpu.make_async_remote_copy(
+                    src_ref=help_send, dst_ref=help_back.at[i],
+                    send_sem=back_sem.at[0, i], recv_sem=back_sem.at[1, i],
+                    device_id=device(last, d), device_id_type=MESH,
+                )
+                back.start()
+                for k in range(chips - 1):
+                    ref = help_in.at[k]
+                    pltpu.make_async_copy(ref, ref, help_sem.at[2, k]).wait()
+                back.wait_send()
+
+    @pl.when(s == 0)
+    def _():
+        @pl.loop(0, micro + 2)
+        def _(t):
+            @pl.when(t < micro)
+            def _():
+                step_project(t - 0)
+
+            @pl.when(t >= 2)
+            def _():
+                step_forward(t - 2)
+
+            @pl.when((t >= 1) & (t < micro + 1))
+            def _():
+                step_weigh(t - 1)
+
+            @pl.when((t >= 1) & (t < micro + 1))
+            def _():
+                step_values(t - 1)
+
+            @pl.when((t >= group) & (t < micro))
+            def _():
+                step_gradient(t)
+
+            @pl.when(t == micro)
+            def _():
+                step_last_gradient()
+
+            @pl.when(t < micro)
+            def _():
+                step_scatter(t - 0)
+
+            @pl.when(t >= 2)
+            def _():
+                step_output(t - 2)
+
+
+    @pl.when((s > 0) & (s < last))
+    def _():
+        @pl.loop(0, micro + 2)
+        def _(t):
+            @pl.when(t < micro)
+            def _():
+                step_project(t - 0)
+
+            @pl.when((t >= 1) & (t < micro + 1))
+            def _():
+                step_weigh(t - 1)
+
+            @pl.when((t >= 1) & (t < micro + 1))
+            def _():
+                step_values(t - 1)
+
+            @pl.when(t >= 2)
+            def _():
+                step_output(t - 2)
+
+            @pl.when(t < micro)
+            def _():
+                step_scatter(t - 0)
+
+            @pl.when((t >= group) & (t < micro))
+            def _():
+                step_gradient(t)
+
+            @pl.when(t == micro)
+            def _():
+                step_last_gradient()
+
+            @pl.when((t >= 1) & (t < micro + 1))
+            def _():
+                step_forward(t - 1)
+
+
+    @pl.when(s == last)
+    def _():
+        @pl.loop(0, micro + 2)
+        def _(t):
+            @pl.when(t < micro)
+            def _():
+                step_project(t - 0)
+
+            @pl.when((t >= 1) & (t < micro))
+            def _():
+                step_weigh(t - 1)
+                step_values(t - 1)
+
+            @pl.when(t >= 2)
+            def _():
+                step_output(t - 2)
+
+            @pl.when(t < micro)
+            def _():
+                step_scatter(t - 0)
+
+            @pl.when((t >= group) & (t < micro))
+            def _():
+                step_gradient(t)
+
+            @pl.when(t == micro - 1)
+            def _():
+                step_weigh(t)
+                step_last_gradient()
+                left_load.start()
+                step_values(t)
+                step_right()
+
+            @pl.when((t >= 1) & (t < micro + 1))
+            def _():
+                step_forward(t - 1)
+
+
+    @pl.when(s < last)
+    def _():
+        left_load.start()
+        step_right()
+
     step_left()
     step_last_right()
+    step_help()
 
     @pl.loop(0, micro)
     def _(m):
@@ -343,6 +503,10 @@
             pltpu.VMEM((chips, share, width), BF16),
             pltpu.VMEM((chips - 1, share, width), BF16),
             pltpu.VMEM((chips - 1, share, width), BF16),
+            pltpu.VMEM((chips - 1, share, width // 4), BF16),
+            pltpu.VMEM((chips - 1, share, width // 4), BF16),
+            pltpu.VMEM((share, width // 4), BF16),
+            pltpu.VMEM((2, share, width // 4), BF16),
             pltpu.VMEM((micro, rows_all, cols), BF16),
             pltpu.VMEM((rows_all, width), F32),
             pltpu.VMEM((half, width), F32),
@@ -357,7 +521,9 @@
             pltpu.SemaphoreType.DMA((6, micro)),
             pltpu.SemaphoreType.DMA((5,)),
             pltpu.SemaphoreType.DMA((2, chips)),
-            pltpu.SemaphoreType.DMA((2, chips - 1)),
+            pltpu.SemaphoreType.DMA((2, chips - 1, 3)),
+            pltpu.SemaphoreType.DMA((3, chips - 1)),
+            pltpu.SemaphoreType.DMA((2, 2)),
         ],
         compiler_params=pltpu.CompilerParams(
             collective_id=0, has_side_effects=True, vmem_limit_bytes=VMEM_BYTES

time: 206 us -> 183 us (0.89)
  Pallas kernels: 199 us -> 175 us
    pallas_call x1, Pallas kernels: 199 us -> 175 us  [relay(): pl.pallas_call(functools.partial(relay_kernel, sections, dp, cols * dp),...]
where the time goes in v2:
time: 183 us; the launch traced here: 182 us
  Pallas kernels  175 us (96%)
  local copies, waits for them, and re-layouts  6.2 us (3%)
    pallas_call x1, Pallas kernels, relay(): pl.pallas_call(functools.partial(relay_kernel, sections, dp, cols * dp),...  175 us
    unnamed x3, local copies, waits for them, and re-layouts  6.2 us

profile of v2, /device:TPU:15, one launch (start us, length us, event | category | flops | bytes accessed | tf_op | source)
XLA Modules:
  0.0 181.6 jit_solution(97012828920942422)
XLA Ops:
  0.6 174.7 %shard_map.94 = (bf16[16,64,2048]{2,1,0:T(8,128)(2,1)S(1)}, f32[2048,1024]{1,0:T(8,128)S(1)}, f32[128,1024]{1,0:T(8,128)S(1)}) custom-call(bf16[16,64,2048]{2,1,0:T(8,128)(2,1)} %bitcast.13, bf16[16,64,1024]{2,1,0:T(8,128)(2,1)} %bitcast.16, bf16[1,2048]{1,0:T(2,128)(2,1)} %gain.1, bf16[2048,1024]{1,0:T(8,128)(2,1)} %bitcast.14, ...), custom_call_target="tpu_custom_call" | custom-call | tf_op jit(solution)/shard_map/pallas_call | solution.py:485
  175.4 2.0 %copy.13 = bf16[1,8,128,2048]{3,2,1,0:T(8,128)(2,1)} copy(bf16[1,8,128,2048]{3,2,1,0:T(8,128)(2,1)S(1)} %bitcast.10) | data formatting | bytes 8388608
  177.4 3.4 %copy.14 = f32[1,2,1024,1024]{3,2,1,0:T(8,128)} copy(f32[1,2,1024,1024]{3,2,1,0:T(8,128)S(1)} %bitcast.9) | data formatting | bytes 16777216
  180.8 0.8 copy.15

commit v3 on v2

--- a/solution.py
+++ b/solution.py
@@ -8,10 +8,15 @@
 from jax.sharding import PartitionSpec as P
 
 BLOCK = 1024
+PIECES = 4
 VMEM_BYTES = 46 * 1024 * 1024
 MESH = pl.DeviceIdType.MESH
 F32 = jnp.float32
 BF16 = jnp.bfloat16
+
+
+def owner_chips(chips):
+    return (chips // 2 - 1, chips // 2) if chips >= 4 else tuple(range(chips))
 
 
 def relay_kernel(
@@ -21,13 +26,14 @@
     grad, scaled, weighted, cot, wv, wo, right_own, right_send, right_recv,
     z_send, z_recv, help_in, help_recv, help_send, help_back,
     xbuf, prod, csum, invs, sq, pair_send, pair_recv, rs_send, rs_recv, vals,
-    send_sem, recv_sem, load_sem, right_sem, z_sem, help_sem, back_sem,
+    send_sem, recv_sem, x_sem, load_sem, right_sem, z_sem, help_sem, back_sem,
 ):
     chips = dp // 2
     micro, rows_all, cols = x_in.shape
     width = wv.shape[1]
     half = rows_all // 2
-    rows = half // chips
+    owners = owner_chips(chips)
+    rows = half // len(owners)
     share = width // dp
     s = lax.axis_index("section")
     d = lax.axis_index("dp")
@@ -42,6 +48,15 @@
     def device(section, index):
         return (section, index)
 
+    piece = cols // PIECES
+
+    def load_x(m):
+        for p in range(PIECES):
+            lanes = pl.ds(p * piece, piece)
+            pltpu.make_async_copy(
+                x_in.at[m, :, lanes], xbuf.at[m, :, lanes], x_sem.at[p, m]
+            ).start()
+
     loads = [
         pltpu.make_async_copy(src, dst, load_sem.at[i])
         for i, (src, dst) in enumerate(((wv_in, wv), (cot_in, cot), (wo_in, wo), (right_in, right_out)))
@@ -50,7 +65,7 @@
 
     @pl.when(s == 0)
     def _():
-        pltpu.make_async_copy(x_in.at[0], xbuf.at[0], recv_sem.at[0, 0]).start()
+        load_x(0)
 
     loads[0].start()
 
@@ -58,7 +73,7 @@
     def _():
         @pl.loop(1, micro)
         def _(m):
-            pltpu.make_async_copy(x_in.at[m], xbuf.at[m], recv_sem.at[0, m]).start()
+            load_x(m)
 
     barrier = pltpu.get_barrier_semaphore()
     for j in range(1, dp):
@@ -80,6 +95,7 @@
                 pl.semaphore_signal(barrier, inc=1, device_id=device(there, d), device_id_type=MESH)
 
             greeted = greeted + jnp.where(s == here, 1, 0)
+
     pl.semaphore_wait(barrier, greeted)
 
     def send(src, dst, phase, m, section, index):
@@ -96,41 +112,62 @@
         pltpu.make_async_copy(ref, ref, send_sem.at[phase, m]).wait()
 
     def step_project(m):
-        wait_in(xbuf.at[m], 0, m)
         total = jnp.zeros((rows_all, 128), F32)
-        for k in range(cols // 128):
-            piece = xbuf[m, :, k * 128:(k + 1) * 128].astype(F32)
-            total = total + piece * piece
-            scaled[m, :, k * 128:(k + 1) * 128] = (
-                piece * gain[:, k * 128:(k + 1) * 128].astype(F32)
-            ).astype(BF16)
-        row = jnp.sum(total.T, axis=0, keepdims=True)
-        sq[m, d] = jnp.broadcast_to(row, (8, rows_all))
-        for j in range(1, dp):
-            send(sq.at[m, d], sq.at[m, d], 1, m, s, lax.rem(d + j, dp))
-
-        @pl.when(m == 0)
-        def _():
-            loads[0].wait()
-            for load in loads[1:]:
-                load.start()
-
-        prod[...] = jnp.dot(scaled[m], wv[...], preferred_element_type=F32)
+        for p in range(PIECES):
+            lanes = pl.ds(p * piece, piece)
+            ref = xbuf.at[m, :, lanes]
+            pltpu.make_async_copy(ref, ref, x_sem.at[p, m]).wait()
+            for k in range(p * piece // 128, (p + 1) * piece // 128):
+                values = xbuf[m, :, k * 128:(k + 1) * 128].astype(F32)
+                total = total + values * values
+                scaled[m, :, k * 128:(k + 1) * 128] = (
+                    values * gain[:, k * 128:(k + 1) * 128].astype(F32)
+                ).astype(BF16)
+            if p == PIECES - 1:
+                row = jnp.sum(total.T, axis=0, keepdims=True)
+                sq[m, d] = jnp.broadcast_to(row, (8, rows_all))
+                for j in range(1, dp):
+                    send(sq.at[m, d], sq.at[m, d], 1, m, s, lax.rem(d + j, dp))
+            if p == 0:
+                @pl.when(m == 0)
+                def _():
+                    loads[0].wait()
+                    for load in loads[1:]:
+                        load.start()
+            product = jnp.dot(scaled[m, :, lanes], wv[lanes, :], preferred_element_type=F32)
+            if p == 0:
+                prod[...] = product
+            else:
+                prod[...] += product
 
         pair_send[m] = prod[pl.ds(pl.multiple_of((1 - c) * half, half), half), :].astype(BF16)
         send(pair_send.at[m], pair_recv.at[m], 2, m, s, partner)
 
+    is_owner = functools.reduce(jnp.logical_or, [z == owner for owner in owners])
+
+    def wait_values(wait, m):
+        @pl.when(is_owner)
+        def _():
+            if len(owners) > 1:
+                wait(vals.at[m, c, pl.ds(0, len(owners) - 1)], 4, m)
+
+        @pl.when(jnp.logical_not(is_owner))
+        def _():
+            wait(vals.at[m, c], 4, m)
+
     def step_forward(m):
-        wait_in(vals.at[m, c, pl.ds(0, chips - 1)], 4, m)
+        wait_values(wait_in, m)
         send(vals.at[m, c], vals.at[m, c], 5, m, s, partner)
 
     def step_scatter(m):
         wait_in(pair_recv.at[m], 2, m)
         csum[...] = prod[pl.ds(pl.multiple_of(c * half, half), half), :] + pair_recv[m].astype(F32)
-        for j in range(1, chips):
-            target = lax.rem(z + j, chips)
-            rs_send[m, j - 1] = csum[pl.ds(pl.multiple_of(target * rows, rows), rows), :].astype(BF16)
-            send(rs_send.at[m, j - 1], rs_recv.at[m, chips - 1 - j], 3, m, s, target * 2 + c)
+        for i, owner in enumerate(owners):
+            @pl.when(z != owner)
+            def _():
+                rs_send[m, i] = csum[i * rows:(i + 1) * rows, :].astype(BF16)
+                slot = lax.rem(z - owner + chips, chips) - 1
+                send(rs_send.at[m, i], rs_recv.at[m, slot], 3, m, s, owner * 2 + c)
 
     def step_output(m):
         wait_in(vals.at[m, 1 - c], 5, m)
@@ -141,20 +178,20 @@
 
         values = vals[m].reshape(rows_all, width)
 
-        for side in range(4):
-            @pl.loop(0, cols // 2048)
-            def _(n):
-                at = pl.ds(pl.multiple_of(side * (cols // 4) + n * 512, 512), 512)
-                out[m, :, at] = (
-                    xbuf[m, :, at].astype(F32)
-                    + jnp.dot(values, wo[:, at], preferred_element_type=F32)
-                ).astype(BF16)
-
-            cut = pl.ds(side * (cols // 4), cols // 4)
+        for p in range(PIECES):
+            lanes = pl.ds(p * piece, piece)
+            out[m, :, lanes] = (
+                xbuf[m, :, lanes].astype(F32)
+                + jnp.dot(values, wo[:, lanes], preferred_element_type=F32)
+            ).astype(BF16)
 
             @pl.when(s < sections - 1)
             def _():
-                send(out.at[m, :, cut], xbuf.at[m, :, cut], 0, m, s + 1, d)
+                pltpu.make_async_remote_copy(
+                    src_ref=out.at[m, :, lanes], dst_ref=xbuf.at[m, :, lanes],
+                    send_sem=send_sem.at[0, m], recv_sem=x_sem.at[p, m],
+                    device_id=device(s + 1, d), device_id_type=MESH,
+                ).start()
 
     def step_weigh(m):
         wait_in(sq.at[m, pl.ds(0, dp - 1)], 1, m)
@@ -169,22 +206,24 @@
         weighted[m] = (invs[:, 0:1] * cot[m].astype(F32)).astype(BF16)
 
     def step_values(m):
-        wait_in(rs_recv.at[m], 3, m)
-        total = csum[pl.ds(pl.multiple_of(z * rows, rows), rows), :]
-        for j in range(chips - 1):
-            total = total + rs_recv[m, j].astype(F32)
-        own = invs[pl.ds(pl.multiple_of(c * half + z * rows, rows), rows), 0:1]
-        vals[m, c, z] = (own * total).astype(BF16)
-        for j in range(1, chips):
-            target = lax.rem(z + j, chips)
-            send(vals.at[m, c, z], vals.at[m, c, z], 4, m, s, target * 2 + c)
+        for i, owner in enumerate(owners):
+            @pl.when(z == owner)
+            def _():
+                wait_in(rs_recv.at[m], 3, m)
+                total = csum[i * rows:(i + 1) * rows, :]
+                for j in range(chips - 1):
+                    total = total + rs_recv[m, j].astype(F32)
+                own = invs[pl.ds(pl.multiple_of(c * half + i * rows, rows), rows), 0:1]
+                vals[m, c, i] = (own * total).astype(BF16)
+                for j in range(1, chips):
+                    target = (owner + j) % chips
+                    send(vals.at[m, c, i], vals.at[m, c, i], 4, m, s, target * 2 + c)
 
     contract_rows = (((0,), (0,)), ((), ()))
-    tile = 256
     group = max(1, 256 // rows_all)
     groups = micro // group
 
-    def gradient_tile(pair, n):
+    def gradient_tile(pair, n, tile):
         at = pl.ds(pl.multiple_of(n * tile, tile), tile)
         left = scaled[pl.ds(pair * group, group), :, at].reshape(group * rows_all, tile)
         right = weighted[pl.ds(pair * group, group)].reshape(group * rows_all, width)
@@ -192,25 +231,22 @@
 
     def step_gradient(t):
         pair = (t - group) // group
-        side = lax.rem(t, group)
-        tiles = cols // tile // group
-
-        @pl.loop(0, tiles)
-        def _(i):
-            at, update = gradient_tile(pair, side * tiles + i)
-
-            @pl.when(pair == 0)
-            def _():
-                acc[at, :] = update
-
-            @pl.when(pair > 0)
-            def _():
-                acc[at, :] += update
+        at, update = gradient_tile(pair, lax.rem(t, group), cols // group)
+
+        @pl.when(pair == 0)
+        def _():
+            acc[at, :] = update
+
+        @pl.when(pair > 0)
+        def _():
+            acc[at, :] += update
 
     def step_last_gradient():
-        @pl.loop(0, cols // tile)
+        tile = cols // 2
+
+        @pl.loop(0, 2)
         def _(n):
-            at, update = gradient_tile(groups - 1, n)
+            at, update = gradient_tile(groups - 1, n, tile)
             grad[at, :] = (acc[at, :] + update).astype(BF16)
 
     def right_product(j):
@@ -265,9 +301,9 @@
     def step_left():
         left_load.wait()
         for block in range(cols // BLOCK):
-            @pl.loop(0, BLOCK // 256)
+            @pl.loop(0, BLOCK // 512)
             def _(n):
-                at = pl.ds(pl.multiple_of(block * BLOCK + n * 256, 256), 256)
+                at = pl.ds(pl.multiple_of(block * BLOCK + n * 512, 512), 512)
                 product = lax.dot_general(
                     grad[at, :], grad[block * BLOCK:(block + 1) * BLOCK, :],
                     (((1,), (1,)), ((), ())), preferred_element_type=F32,
@@ -464,8 +500,15 @@
     def _(m):
         wait_out(sq.at[m, pl.ds(0, dp - 1)], 1, m)
         wait_out(pair_send.at[m], 2, m)
-        wait_out(rs_send.at[m], 3, m)
-        wait_out(vals.at[m, c, pl.ds(0, chips - 1)], 4, m)
+        for owner in owners:
+            @pl.when(z != owner)
+            def _():
+                wait_out(rs_send.at[m, 0], 3, m)
+
+        @pl.when(is_owner)
+        def _():
+            wait_out(rs_recv.at[m], 4, m)
+
         wait_out(vals.at[m, c], 5, m)
 
         @pl.when(s < sections - 1)
@@ -478,7 +521,7 @@
     width = wv.shape[1]
     chips = dp // 2
     half = rows_all // 2
-    rows = half // chips
+    rows = half // len(owner_chips(chips))
     share = width // dp
     vmem = pl.BlockSpec(memory_space=pltpu.VMEM)
     anywhere = pl.BlockSpec(memory_space=pl.ANY)
@@ -514,11 +557,12 @@
             pltpu.VMEM((micro, dp, 8, rows_all), F32),
             pltpu.VMEM((micro, half, width), BF16),
             pltpu.VMEM((micro, half, width), BF16),
+            pltpu.VMEM((micro, half // rows, rows, width), BF16),
             pltpu.VMEM((micro, chips - 1, rows, width), BF16),
-            pltpu.VMEM((micro, chips - 1, rows, width), BF16),
-            pltpu.VMEM((micro, 2, chips, rows, width), BF16),
+            pltpu.VMEM((micro, 2, half // rows, rows, width), BF16),
             pltpu.SemaphoreType.DMA((6, micro)),
             pltpu.SemaphoreType.DMA((6, micro)),
+            pltpu.SemaphoreType.DMA((PIECES, micro)),
             pltpu.SemaphoreType.DMA((5,)),
             pltpu.SemaphoreType.DMA((2, chips)),
             pltpu.SemaphoreType.DMA((2, chips - 1, 3)),
@@ -531,6 +575,30 @@
     )(x_in, cot, gain, wv, wo, left, right)
 
 
+def store_kernel(out, left, right, out_hbm, left_hbm, right_hbm, sem):
+    copies = [
+        pltpu.make_async_copy(src, dst, sem.at[i])
+        for i, (src, dst) in enumerate(((left, left_hbm), (out, out_hbm), (right, right_hbm)))
+    ]
+    for copy in copies:
+        copy.start()
+    for copy in copies:
+        copy.wait()
+
+
+def store(*arrays):
+    vmem = pl.BlockSpec(memory_space=pltpu.VMEM)
+    anywhere = pl.BlockSpec(memory_space=pl.ANY)
+    return pl.pallas_call(
+        store_kernel,
+        out_shape=tuple(jax.ShapeDtypeStruct(a.shape, a.dtype) for a in arrays),
+        in_specs=[vmem] * 3,
+        out_specs=(anywhere,) * 3,
+        scratch_shapes=[pltpu.SemaphoreType.DMA((3,))],
+        compiler_params=pltpu.CompilerParams(vmem_limit_bytes=1024 * 1024),
+    )(*[pltpu.with_memory_space_constraint(a, pltpu.VMEM) for a in arrays])
+
+
 def on_device(inputs, cotangent, norm_gain, value_weight, output_weight, left_old, right_old):
     sections = lax.axis_size("section")
     dp = lax.axis_size("dp")
@@ -539,10 +607,10 @@
     chips = dp // 2
     split = 2 if rows_all // dp >= 16 else 1
     chunked = (micro * split, rows_all // split)
-    outputs, left_new, right_new = relay(
+    outputs, left_new, right_new = store(*relay(
         sections, dp, inputs.reshape(chunked + (cols,)), cotangent[0].reshape(chunked + (width,)),
         norm_gain, value_weight[0], output_weight[0], left_old.reshape(cols, width), right_old[0],
-    )
+    ))
     outputs = outputs.reshape((1, micro, rows_all, cols))
     return (outputs, left_new.reshape(left_old.shape), right_new[None])
 

time: 183 us -> 180 us (0.984)
  local copies, waits for them, and re-layouts: 6.2 us -> 0 us
  Pallas kernels: 175 us -> 177 us
    unnamed x3 -> x0, local copies, waits for them, and re-layouts: 6.2 us -> none
    pallas_call x0 -> x1, Pallas kernels: none -> 4.84 us  [store(): pl.pallas_call(store_kernel, out_shape=tuple((jax.ShapeDtypeStruct(a.shap...]
    pallas_call x1, Pallas kernels: 175 us -> 173 us  [relay(): pl.pallas_call(functools.partial(relay_kernel, sections, dp, cols * dp),...]
where the time goes in v3:
time: 180 us; the launch traced here: 178 us
  Pallas kernels  177 us (98%)
    pallas_call x1, Pallas kernels, relay(): pl.pallas_call(functools.partial(relay_kernel, sections, dp, cols * dp),...  173 us
    pallas_call x1, Pallas kernels, store(): pl.pallas_call(store_kernel, out_shape=tuple((jax.ShapeDtypeStruct(a.shap...  4.84 us

profile of v3, /device:TPU:15, one launch (start us, length us, event | category | flops | bytes accessed | tf_op | source)
XLA Modules:
  0.0 178.3 jit_solution(1763254843465395455)
XLA Ops:
  0.6 172.6 %shard_map.94 = (bf16[16,64,2048]{2,1,0:T(8,128)(2,1)S(1)}, f32[2048,1024]{1,0:T(8,128)S(1)}, f32[128,1024]{1,0:T(8,128)S(1)}) custom-call(bf16[16,64,2048]{2,1,0:T(8,128)(2,1)} %bitcast.10, bf16[16,64,1024]{2,1,0:T(8,128)(2,1)} %bitcast.13, bf16[1,2048]{1,0:T(2,128)(2,1)} %gain.1, bf16[2048,1024]{1,0:T(8,128)(2,1)} %bitcast.11, ...), custom_call_target="tpu_custom_call" | custom-call | tf_op jit(solution)/shard_map/pallas_call | solution.py:528
  173.3 4.8 %shard_map.95 = (bf16[16,64,2048]{2,1,0:T(8,128)(2,1)}, f32[2048,1024]{1,0:T(8,128)}, f32[128,1024]{1,0:T(8,128)}) custom-call(bf16[16,64,2048]{2,1,0:T(8,128)(2,1)S(1)} %get-tuple-element.9.out, f32[2048,1024]{1,0:T(8,128)S(1)} %get-tuple-element.10.left, f32[128,1024]{1,0:T(8,128)S(1)} %get-tuple-element.11.right), custom_call_target="tpu_custom_call" | custom-call | tf_op jit(solution)/shard_map/pallas_call | solution.py:592

commit v4 on v3

--- a/solution.py
+++ b/solution.py
@@ -42,8 +42,8 @@
     partner = z * 2 + (1 - c)
     last = sections - 1
     helpers = (last ^ 2, last ^ 3) if sections % 4 == 0 else ()
-    own_cols = width // 2 if helpers else width
-    slice_cols = (width - own_cols) // max(1, len(helpers))
+    own_cols = 5 * width // 8 if helpers else width
+    slices = (width // 4, width // 8)
 
     def device(section, index):
         return (section, index)
@@ -280,11 +280,11 @@
         own = pl.ds(0, own_cols)
         scatter(own, z_recv.at[slot, :, own], 0, z_sem.at[1, slot, 0], s)
         for i, h in enumerate(helpers):
-            cut = pl.ds(own_cols + i * slice_cols, slice_cols)
+            cut = pl.ds(own_cols + sum(slices[:i]), slices[i])
 
             @pl.when(s == last)
             def _():
-                scatter(cut, help_in.at[j - 1], 1 + i, help_sem.at[0, j - 1], h, d)
+                scatter(cut, help_in.at[j - 1, :, pl.ds(0, slices[i])], 1 + i, help_sem.at[0, j - 1], h, d)
 
             @pl.when(s < last)
             def _():
@@ -325,14 +325,14 @@
 
         gather(pl.ds(0, own_cols), 0)
         for i, h in enumerate(helpers):
-            cut = pl.ds(own_cols + i * slice_cols, slice_cols)
+            cut = pl.ds(own_cols + sum(slices[:i]), slices[i])
 
             @pl.when(s == last)
             def _():
-                ref = help_back.at[i]
+                ref = help_back.at[i, :, pl.ds(0, slices[i])]
                 pltpu.make_async_copy(ref, ref, back_sem.at[1, i]).wait()
                 total = right_own[0, c, :, cut] + right_recv[0, :, cut].astype(F32)
-                right_out[:, cut] += (total + help_back[i].astype(F32)) * scale
+                right_out[:, cut] += (total + help_back[i, :, :slices[i]].astype(F32)) * scale
 
             @pl.when(s < last)
             def _():
@@ -342,7 +342,7 @@
             pltpu.make_async_copy(right_send.at[j], right_send.at[j], right_sem.at[0, j]).wait()
         for j in range(chips - 1):
             for part in range(1 + len(helpers)):
-                ref = z_send.at[j, :, pl.ds(0, slice_cols if part else own_cols)]
+                ref = z_send.at[j, :, pl.ds(0, slices[part - 1] if part else own_cols)]
                 pltpu.make_async_copy(ref, ref, z_sem.at[0, j, part]).wait()
 
     def step_help():
@@ -350,28 +350,29 @@
             @pl.when(s == h)
             def _():
                 for j in range(1, chips):
-                    ref = help_in.at[j - 1]
+                    ref = help_in.at[j - 1, :, pl.ds(0, slices[i])]
                     pltpu.make_async_copy(ref, ref, help_sem.at[0, j - 1]).wait()
                     pltpu.make_async_remote_copy(
-                        src_ref=ref, dst_ref=help_recv.at[chips - 1 - j],
+                        src_ref=ref, dst_ref=help_recv.at[chips - 1 - j, :, pl.ds(0, slices[i])],
                         send_sem=help_sem.at[2, j - 1], recv_sem=help_sem.at[1, chips - 1 - j],
                         device_id=device(s, lax.rem(z + j, chips) * 2 + c), device_id_type=MESH,
                     ).start()
                 total = None
                 for k in range(chips - 1):
-                    ref = help_recv.at[k]
+                    ref = help_recv.at[k, :, pl.ds(0, slices[i])]
                     pltpu.make_async_copy(ref, ref, help_sem.at[1, k]).wait()
-                    piece = help_recv[k].astype(F32)
+                    piece = help_recv[k, :, :slices[i]].astype(F32)
                     total = piece if total is None else total + piece
-                help_send[...] = total.astype(BF16)
+                help_send[:, :slices[i]] = total.astype(BF16)
                 back = pltpu.make_async_remote_copy(
-                    src_ref=help_send, dst_ref=help_back.at[i],
+                    src_ref=help_send.at[:, pl.ds(0, slices[i])],
+                    dst_ref=help_back.at[i, :, pl.ds(0, slices[i])],
                     send_sem=back_sem.at[0, i], recv_sem=back_sem.at[1, i],
                     device_id=device(last, d), device_id_type=MESH,
                 )
                 back.start()
                 for k in range(chips - 1):
-                    ref = help_in.at[k]
+                    ref = help_in.at[k, :, pl.ds(0, slices[i])]
                     pltpu.make_async_copy(ref, ref, help_sem.at[2, k]).wait()
                 back.wait_send()
 

time: 180 us -> 181 us (level)
  Pallas kernels: 177 us -> 179 us
    pallas_call x1, Pallas kernels: 173 us -> 175 us  [relay(): pl.pallas_call(functools.partial(relay_kernel, sections, dp, cols * dp),...]
where the time goes in v4:
time: 181 us; the launch traced here: 180 us
  Pallas kernels  179 us (99%)
    pallas_call x1, Pallas kernels, relay(): pl.pallas_call(functools.partial(relay_kernel, sections, dp, cols * dp),...  175 us
    pallas_call x1, Pallas kernels, store(): pl.pallas_call(store_kernel, out_shape=tuple((jax.ShapeDtypeStruct(a.shap...  4.84 us

profile of v4, /device:TPU:15, one launch (start us, length us, event | category | flops | bytes accessed | tf_op | source)
XLA Modules:
  0.0 180.3 jit_solution(15104522747349481072)
XLA Ops:
  0.6 174.7 %shard_map.94 = (bf16[16,64,2048]{2,1,0:T(8,128)(2,1)S(1)}, f32[2048,1024]{1,0:T(8,128)S(1)}, f32[128,1024]{1,0:T(8,128)S(1)}) custom-call(bf16[16,64,2048]{2,1,0:T(8,128)(2,1)} %bitcast.10, bf16[16,64,1024]{2,1,0:T(8,128)(2,1)} %bitcast.13, bf16[1,2048]{1,0:T(2,128)(2,1)} %gain.1, bf16[2048,1024]{1,0:T(8,128)(2,1)} %bitcast.11, ...), custom_call_target="tpu_custom_call" | custom-call | tf_op jit(solution)/shard_map/pallas_call | solution.py:529
  175.3 4.8 %shard_map.95 = (bf16[16,64,2048]{2,1,0:T(8,128)(2,1)}, f32[2048,1024]{1,0:T(8,128)}, f32[128,1024]{1,0:T(8,128)}) custom-call(bf16[16,64,2048]{2,1,0:T(8,128)(2,1)S(1)} %get-tuple-element.9.out, f32[2048,1024]{1,0:T(8,128)S(1)} %get-tuple-element.10.left, f32[128,1024]{1,0:T(8,128)S(1)} %get-tuple-element.11.right), custom_call_target="tpu_custom_call" | custom-call | tf_op jit(solution)/shard_map/pallas_call | solution.py:593
